TPU v7x, 32 devices: a whole 2x2x4 slice. The times are simulated.
32 devices in a mesh: tok: 4 (over y, x), row: 2 (over core), col: 4 (over z).
Axes of the slice: x: 2, y: 2, z: 4, core: 2. Of those that a mesh axis runs over, the one named last changes fastest.
Arguments:
- activations: bfloat16 [2048, 4096], P(('tok', 'col'), 'row'), may hold values from -6 to 6
- grads_t: bfloat16 [4, 7392, 2048], P(None, 'col', ('tok', 'row')), may hold values from -0.14941406 to 0.14941406
Outputs:
- weight_grad: float32 [4, 7392, 4096], P('tok', 'col', 'row')
All inputs are finite; a program needn't handle non-finite values.
Results may differ from a plain program's by a relative error of at most 0.0003.
Values may be sent and summed in bfloat16 or wider, within the bound.
A program may use at most 128 MiB of HBM per device.

v0:
```python
import jax
import jax.numpy as jnp
from jax import lax
from jax.sharding import PartitionSpec as P


def body(activations, grads_t):
    groups, units, own = grads_t.shape
    grads_all = lax.all_gather(grads_t, "row", axis=2, tiled=True)
    acts_all = lax.all_gather(activations, "col", axis=0, tiled=True)
    width = acts_all.shape[1]
    flat = grads_all.reshape(groups * units, grads_all.shape[2])
    tile = jnp.dot(flat, acts_all, preferred_element_type=jnp.float32)
    result = lax.psum_scatter(
        tile.reshape(groups, units, width), "tok", scatter_dimension=0, tiled=True
    )
    return result


def solution(mesh):
    return jax.shard_map(
        body,
        mesh=mesh,
        in_specs=(P(("tok", "col"), "row"), P(None, "col", ("tok", "row"))),
        out_specs=P("tok", "col", "row"),
        check_vma=False,
    )
```

profile of v0, /device:TPU:1, one launch (start us, length us, event | category | flops | bytes accessed | tf_op | source)
XLA Modules:
  0.0 616.1 jit_solution(4035724320007954552)
XLA Ops:
  6.5 0.0 all-gather.5.cloned.1.call-start
  6.5 0.7 all-gather.5.cloned.1.call-update
  7.3 0.0 all-gather.3.cloned.1.call-start
  7.3 0.7 all-gather.3.cloned.1.call-update
  8.0 0.0 reduce-scatter.4.cloned.1.call-start
  8.1 48.4 %all-gather.5.cloned.1.call-done = bf16[512,2048]{1,0:T(8,128)(2,1)} async-done(((bf16[128,2048]{1,0:T(8,128)(2,1)}), bf16[512,2048]{1,0:T(8,128)(2,1)}) %all-gather.5.cloned.1.call-update) | async-done | bytes 2097168 | tf_op jit(solution)/shard_map/all_gather | solution.py:10
  56.5 18.0 %all-gather.3.cloned.1.call-done = bf16[4,1848,512]{2,1,0:T(8,128)(2,1)} async-done(((bf16[4,1848,256]{2,1,0:T(8,128)(2,1)}), bf16[4,1848,512]{2,1,0:T(8,128)(2,1)}) %all-gather.3.cloned.1.call-update) | async-done | bytes 7569424 | tf_op jit(solution)/shard_map/all_gather | solution.py:9
  74.5 27.8 %fusion = f32[4,1848,2048]{2,1,0:T(8,128)} fusion(bf16[4,1848,512]{2,1,0:T(8,128)(2,1)} %all-gather.3.cloned.1.call-done, bf16[512,2048]{1,0:T(8,128)(2,1)} %all-gather.5.cloned.1.call-done), kind=kOutput, calls=%fused_computation | convolution fusion | flops 15502147584 | bytes 70221824 | tf_op jit(solution)/shard_map/dot_general | solution.py:13
  102.3 0.0 reduce-scatter.4.cloned.1.call-update
  102.3 507.2 %reduce-scatter.4.cloned.1.call-done = f32[1,1848,2048]{2,1,0:T(8,128)} async-done(((f32[4,1848,2048]{2,1,0:T(8,128)}), f32[1,1848,2048]{2,1,0:T(8,128)}) %reduce-scatter.4.cloned.1.call-update) | async-done | bytes 15138832
Async XLA Ops:
  6.5 50.0 %all-gather.5.cloned.1.call-start = ((), (), s32[]{:S(2)}) async-start(), calls=%async_computation.2 | async-start | bytes 2621440 | tf_op jit(solution)/shard_map/all_gather | solution.py:10
  7.3 67.2 %all-gather.3.cloned.1.call-start = ((), (), s32[]{:S(2)}) async-start(), calls=%async_computation.1 | async-start | bytes 11354112 | tf_op jit(solution)/shard_map/all_gather | solution.py:9
  8.0 601.5 %reduce-scatter.4.cloned.1.call-start = ((), (), s32[]{:S(2)}) async-start(), calls=%async_computation.3 | async-start | bytes 75694080
Sparse Core Ops, SparseCore 0:
  8.9 47.5 all-gather.4
  58.0 16.4 all-gather.2
  102.4 507.0 reduce-scatter.3
where the time goes:
time: 617 us; the launch traced here: 616 us
  waiting for transfers between devices  575 us (93%)
  matrix products  27.8 us (5%)
  between operations  13.1 us (2%)
    unnamed x4, waiting for transfers between devices  509 us
    all_gather x1, waiting for transfers between devices, body(): acts_all = lax.all_gather(activations, 'col', axis=0, tiled=True)  48.4 us
    dot_general x1, matrix products, body(): tile = jnp.dot(flat, acts_all, preferred_element_type=jnp.float32)  27.8 us
    all_gather x1, waiting for transfers between devices, body(): grads_all = lax.all_gather(grads_t, 'row', axis=2, tiled=True)  18 us
  transfers between devices with their start and end apart: 3, of which 3 were waited for; matrix products, arithmetic and copies ran while one was open for 0% of the time, Pallas kernels for 0%

commit v1 on v0

v1 whole, which is shorter than its diff:
```python
import jax
import jax.numpy as jnp
from jax import lax
from jax.sharding import PartitionSpec as P


def body(activations, grads_t):
    groups, units, own = grads_t.shape
    mine = lax.all_to_all(grads_t, "tok", split_axis=0, concat_axis=0, tiled=True)
    mine = lax.all_gather(mine, "row", axis=1, tiled=False)
    acts_all = lax.all_gather(activations, "col", axis=0, tiled=True)
    acts_all = lax.all_gather(acts_all, "tok", axis=0, tiled=True)
    flat = mine.transpose(2, 0, 1, 3).reshape(units, mine.size // units)
    tile = jnp.dot(flat, acts_all, preferred_element_type=jnp.float32)
    return tile[None]


def solution(mesh):
    return jax.shard_map(
        body,
        mesh=mesh,
        in_specs=(P(("tok", "col"), "row"), P(None, "col", ("tok", "row"))),
        out_specs=P("tok", "col", "row"),
        check_vma=False,
    )
```

time: 617 us -> 197 us (0.32)
  waiting for transfers between devices: 575 us -> 100 us
  blocking collectives: 0 us -> 49.1 us
  local copies, waits for them, and re-layouts: 0 us -> 10.3 us
    unnamed x4 -> x3, waiting for transfers between devices: 509 us -> 1.38 us
    all_gather x1 -> x2, waiting for transfers between devices: 18 us -> 98.9 us  [the longest x1 79.7 us: body(): acts_all = lax.all_gather(acts_all, 'tok', axis=0, tiled=True)]
    all_to_all x0 -> x1, blocking collectives: none -> 49.1 us  [body(): lax.all_to_all(grads_t, 'tok', split_axis=0, concat_axis=0, tiled=True)]
    all_gather x1, waiting for transfers between devices: 48.4 us -> 0.02 us  [body(): acts_all = lax.all_gather(activations, 'col', axis=0, tiled=True)]
    all_gather x0 -> x1, local copies, waits for them, and re-layouts: none -> 10.3 us  [body(): mine = lax.all_gather(mine, 'row', axis=1, tiled=False)]
  transfers between devices with their start and end apart: 3 -> 3, of which waited for: 3 -> 2; matrix products, arithmetic and copies ran while one was open for 0% -> 5% of each run, Pallas kernels for 0% -> 0%
where the time goes in v1:
time: 197 us; the launch traced here: 195 us
  waiting for transfers between devices  100 us (51%)
  blocking collectives  49.1 us (25%)
  matrix products  22.3 us (11%)
  between operations  13.1 us (7%)
  local copies, waits for them, and re-layouts  10.3 us (5%)
    all_gather x1, waiting for transfers between devices, body(): acts_all = lax.all_gather(acts_all, 'tok', axis=0, tiled=True)  79.7 us
    all_to_all x1, blocking collectives, body(): lax.all_to_all(grads_t, 'tok', split_axis=0, concat_axis=0, tiled=True)  49.1 us
    dot_general x1, matrix products, body(): tile = jnp.dot(flat, acts_all, preferred_element_type=jnp.float32)  22.3 us
    all_gather x1, waiting for transfers between devices, body(): mine = lax.all_gather(mine, 'row', axis=1, tiled=False)  19.2 us
    all_gather x1, local copies, waits for them, and re-layouts, body(): mine = lax.all_gather(mine, 'row', axis=1, tiled=False)  10.3 us
  transfers between devices with their start and end apart: 3, of which 2 were waited for; matrix products, arithmetic and copies ran while one was open for 5% of the time, Pallas kernels for 0%

profile of v1, /device:TPU:1, one launch (start us, length us, event | category | flops | bytes accessed | tf_op | source)
XLA Modules:
  0.0 195.3 jit_solution(12138693285558860442)
XLA Ops:
  6.5 0.0 all-gather.5.cloned.1.call-start
  6.5 0.7 all-gather.5.cloned.1.call-update
  7.3 0.0 all-gather.9.cloned.1.call-start
  7.3 49.1 %all_to_all.5 = bf16[4,1848,256]{2,1,0:T(8,128)(2,1)} all-to-all(bf16[4,1848,256]{2,1,0:T(8,128)(2,1)} %param.3), channel_id=1, replica_groups=mesh['tok'=4,'row'=2,'col'=4] {'tok'}, dimensions={0} | all-to-all | bytes 7569408 | tf_op jit(solution)/shard_map/all_to_all | solution.py:9
  56.4 0.0 all-gather.9.cloned.1.call-update
  56.5 0.0 all-gather.7.cloned.1.call-start
  56.5 0.0 all-gather.5.cloned.1.call-done
  56.5 0.7 all-gather.7.cloned.1.call-update
  57.2 19.2 %all-gather.9.cloned.1.call-done = bf16[4,3696,256]{2,1,0:T(8,128)(2,1)} async-done(((bf16[4,1848,256]{2,1,0:T(8,128)(2,1)}), bf16[4,3696,256]{2,1,0:T(8,128)(2,1)}) %all-gather.9.cloned.1.call-update) | async-done | bytes 7569424 | tf_op jit(solution)/shard_map/all_gather | solution.py:10
  76.4 10.3 %copy.3 = bf16[4,2,1848,256]{2,3,1,0:T(8,128)(2,1)} copy(bf16[4,2,1848,256]{3,2,1,0:T(8,128)(2,1)} %bitcast.9) | data formatting | bytes 15138816 | tf_op jit(solution)/shard_map/all_gather | solution.py:10
  86.7 79.7 %all-gather.7.cloned.1.call-done = bf16[2048,2048]{1,0:T(8,128)(2,1)} async-done(((bf16[512,2048]{1,0:T(8,128)(2,1)}), bf16[2048,2048]{1,0:T(8,128)(2,1)}) %all-gather.7.cloned.1.call-update) | async-done | bytes 8388624 | tf_op jit(solution)/shard_map/all_gather | solution.py:12
  166.4 22.3 %convolution_bitcast_fusion = f32[1,1848,2048]{2,1,0:T(8,128)} fusion(bf16[1848,2048]{0,1:T(8,128)(2,1)} %bitcast.8, bf16[2048,2048]{1,0:T(8,128)(2,1)} %all-gather.7.cloned.1.call-done), kind=kOutput, calls=%fused_computation | convolution fusion | flops 15502147584 | bytes 31096832 | tf_op jit(solution)/shard_map/dot_general | solution.py:14
Async XLA Ops:
  6.5 50.0 %all-gather.5.cloned.1.call-start = ((), (), s32[]{:S(2)}) async-start(), calls=%async_computation.1 | async-start | bytes 2621440 | tf_op jit(solution)/shard_map/all_gather | solution.py:11
  7.3 69.2 %all-gather.9.cloned.1.call-start = ((), (), s32[]{:S(2)}) async-start(), calls=%async_computation.3 | async-start | bytes 11354112 | tf_op jit(solution)/shard_map/all_gather | solution.py:10
  56.5 109.9 %all-gather.7.cloned.1.call-start = ((), (), s32[]{:S(2)}) async-start(), calls=%async_computation.2 | async-start | bytes 10485760 | tf_op jit(solution)/shard_map/all_gather | solution.py:12
Sparse Core Ops, SparseCore 0:
  8.9 47.5 all-gather.4
  58.0 18.3 all-gather.8
  78.3 88.0 all-gather.6

commit v2 on v1

v2 whole, which is shorter than its diff:
```python
import functools

import jax
import jax.numpy as jnp
from jax import lax
from jax.experimental import pallas as pl
from jax.experimental.pallas import tpu as pltpu
from jax.sharding import PartitionSpec as P

MESH = pl.DeviceIdType.MESH


def ring_map(place, n):
    if n % 4:
        return place
    return place + ((place % 4) // 2) * (1 - 2 * (place % 2))


def kernel(n, m, acts, grads, out, first, last, held, total,
           local_sem, zsend, zrecv, rsend, rrecv, gsend, grecv, psend, out_sem):
    k, r, c = lax.axis_index("tok"), lax.axis_index("row"), lax.axis_index("col")
    place = ring_map(k, n)
    rows, wide = acts.shape
    quarter = wide // 4
    chunk = grads.shape[2]
    up, down = c + 1 < m, c > 0
    reach = ((n // 2, n - 1 - n // 2), (n - 1 - n // 2, n // 2))
    hops = n // 2

    def member(offset):
        return ring_map((place + offset + 2 * n) % n, n)

    barrier = pltpu.get_barrier_semaphore()
    for j in range(1, n):
        pl.semaphore_signal(barrier, inc=1, device_id={"tok": (k + j) % n}, device_id_type=MESH)
    pl.semaphore_signal(barrier, inc=1, device_id={"row": 1 - r}, device_id_type=MESH)

    @pl.when(up)
    def _():
        pl.semaphore_signal(barrier, inc=1, device_id={"col": c + 1}, device_id_type=MESH)

    @pl.when(down)
    def _():
        pl.semaphore_signal(barrier, inc=1, device_id={"col": c - 1}, device_id_type=MESH)

    def span(tok, col):
        return pl.ds(pl.multiple_of((tok * m + col) * rows, rows), rows)

    own = span(k, c)
    loads = []
    for q in range(4):
        dst = (first, last)[q // 2].at[q % 2, own, :]
        loads.append(pltpu.make_async_copy(acts.at[:, pl.ds(q * quarter, quarter)], dst, local_sem.at[q]))
    mine = pltpu.make_async_copy(grads.at[k], held.at[k, r], local_sem.at[4])
    for load in loads[2:] + loads[:2] + [mine]:
        load.start()
    for load in loads:
        load.wait()

    @pl.when(up & down)
    def _():
        pl.semaphore_wait(barrier, n + 2)

    @pl.when(jnp.logical_not(up & down))
    def _():
        pl.semaphore_wait(barrier, n + 1)

    def z_copy(item, tok, col, way):
        buf = first if isinstance(item, int) and item == 0 else last
        where = buf.at[:, span(tok, col), :]
        return pltpu.make_async_remote_copy(
            where, where, zsend.at[way, item, col], zrecv.at[item, col],
            device_id={"col": c + 1 - 2 * way}, device_id_type=MESH)

    def z_start(item, tok):
        @pl.when(up)
        def _():
            z_copy(item, tok, c, 0).start()

        @pl.when(down)
        def _():
            z_copy(item, tok, c, 1).start()

    def z_round(s, item, tok):
        below, above = c - 1 - s, c + 1 + s

        @pl.when(below >= 0)
        def _():
            z_copy(item, tok, below, 0).wait_recv()

            @pl.when(up)
            def _():
                z_copy(item, tok, below, 0).start()

        @pl.when(above < m)
        def _():
            z_copy(item, tok, above, 1).wait_recv()

            @pl.when(down)
            def _():
                z_copy(item, tok, above, 1).start()

    def ring_copy(line, col, offset, half, way):
        buf = last if isinstance(line, int) and line == m else first
        tok = member(offset)
        where = buf.at[half, span(tok, col), :]
        return pltpu.make_async_remote_copy(
            where, where, rsend.at[way, line, tok, half], rrecv.at[line, tok, half],
            device_id={"tok": member(1 - 2 * way)}, device_id_type=MESH)

    def ring_start(line, col):
        for half in range(2):
            for way in range(2):
                which = half if way == 0 else 1 - half
                if reach[which][way] >= 1:
                    ring_copy(line, col, 0, which, way).start()

    def ring_step(line, col, t):
        for half in range(2):
            for way in range(2):
                which = half if way == 0 else 1 - half
                if reach[which][way] >= t:
                    offset = -t if way == 0 else t
                    ring_copy(line, col, offset, which, way).wait_recv()
                    if reach[which][way] > t:
                        ring_copy(line, col, offset, which, way).start()

    def ring_sent(line, col):
        for half in range(2):
            for way in range(2):
                for t in range(reach[half][way]):
                    ring_copy(line, col, -t if way == 0 else t, half, way).wait_send()

    def at_distance(d, do):
        @pl.when(c - d >= 0)
        def _():
            do(c - d, c - d)

        @pl.when((c + d < m) & (d > 0))
        def _():
            do(c + d, c + d)

    def g_send(j):
        to = (k + j) % n
        return pltpu.make_async_remote_copy(
            grads.at[to], held.at[k, r], gsend.at[j], grecv.at[k, r],
            device_id={"tok": to}, device_id_type=MESH)

    def g_recv(tok):
        where = held.at[tok, r]
        return pltpu.make_async_remote_copy(
            where, where, gsend.at[0], grecv.at[tok, r],
            device_id={"row": 1 - r}, device_id_type=MESH)

    def partner(tok, side):
        where = held.at[tok, side]
        return pltpu.make_async_remote_copy(
            where, where, psend.at[tok], grecv.at[tok, side],
            device_id={"row": 1 - r}, device_id_type=MESH)

    ring_start(m, c)
    z_start(0, k)
    z_start(1, k)
    ring_start(c, c)
    mine.wait()
    partner(k, r).start()
    for t in range(1, hops + 1):
        ring_step(m, c, t)
        if t == 1:
            for j in sorted(range(1, n), key=lambda j: (min(j, n - j), j)):
                g_send(j).start()
        z_start(1 + (n - t), member(-t))
        if 2 * t != n:
            z_start(1 + t, member(t))
        if t == 1:
            total[...] = jnp.zeros_like(total)

    def item_order():
        order = [0]
        for t in range(1, hops + 1):
            order.append(n - t)
            if 2 * t != n:
                order.append(t)
        return order

    def whole_round(s):
        z_round(s, 0, k)
        at_distance(s + 1, ring_start)
        for j in item_order():
            z_round(s, 1 + j, member(j))

    def compute(buf, base, tok, side):
        at = pl.ds(pl.multiple_of((tok * 2 + side) * chunk, chunk), chunk)
        step = min(256, quarter)
        for half in range(2):
            @pl.loop(0, quarter // step)
            def _(i):
                cols = pl.ds(pl.multiple_of(i * step, step), step)
                outc = pl.ds(pl.multiple_of((base + half) * quarter + i * step, step), step)
                total[:, outc] += jnp.dot(
                    held[tok, side], buf[half, at, cols], preferred_element_type=jnp.float32)

    @pl.loop(0, m - 2)
    def _(s):
        whole_round(s)

    for j in sorted(range(1, n), key=lambda j: (min(j, n - j), j)):
        tok = (k + n - j) % n
        g_recv(tok).wait_recv()
        partner(tok, r).start()

    near = (2 * c) // m

    @pl.loop(0, m - 1)
    def _(d):
        at_distance(d, functools.partial(ring_step, t=1))

    @pl.loop(0, n)
    def _(j):
        partner((k + j) % n, 1 - r).wait_recv()

    @pl.loop(0, n)
    def _(j):
        compute(last, 2, j, near)

    z_round(m - 2, 0, k)
    at_distance(m - 1, ring_start)
    at_distance(m - 1, functools.partial(ring_step, t=1))
    for j in item_order():
        z_round(m - 2, 1 + j, member(j))
    for t in range(2, hops + 1):
        @pl.loop(0, m)
        def _(d):
            at_distance(d, functools.partial(ring_step, t=t))

    @pl.loop(0, n)
    def _(j):
        compute(last, 2, j, 1 - near)

    @pl.loop(0, 2 * n)
    def _(j):
        compute(first, 0, j // 2, j % 2)

    writes = pltpu.make_async_copy(total, out.at[0], out_sem)
    writes.start()

    for j in range(1, n):
        g_send(j).wait_send()

    @pl.loop(0, n)
    def _(j):
        partner(j, r).wait_send()

    ring_sent(m, c)

    @pl.loop(0, m)
    def _(d):
        at_distance(d, ring_sent)

    def z_sent(item, tok):
        @pl.loop(0, m)
        def _(col):
            @pl.when((col <= c) & up)
            def _():
                z_copy(item, tok, col, 0).wait_send()

            @pl.when((col >= c) & down)
            def _():
                z_copy(item, tok, col, 1).wait_send()

    z_sent(0, k)
    for j in range(n):
        z_sent(1 + j, member(j))
    writes.wait()


def body(n, m, activations, grads_t):
    _, units, chunk = grads_t.shape
    rows, wide = activations.shape
    tokens = rows * n * m
    dma = pltpu.SemaphoreType.DMA
    return pl.pallas_call(
        functools.partial(kernel, n, m),
        out_shape=jax.ShapeDtypeStruct((1, units, wide), jnp.float32),
        in_specs=[pl.BlockSpec(memory_space=pl.ANY)] * 2,
        out_specs=pl.BlockSpec(memory_space=pl.ANY),
        scratch_shapes=[
            pltpu.VMEM((2, tokens, wide // 4), jnp.bfloat16),
            pltpu.VMEM((2, tokens, wide // 4), jnp.bfloat16),
            pltpu.VMEM((n, 2, units, chunk), jnp.bfloat16),
            pltpu.VMEM((units, wide), jnp.float32),
            dma((5,)),
            dma((2, n + 1, m)),
            dma((n + 1, m)),
            dma((2, m + 1, n, 2)),
            dma((m + 1, n, 2)),
            dma((n,)),
            dma((n, 2)),
            dma((n,)),
            dma,
        ],
        compiler_params=pltpu.CompilerParams(
            collective_id=0, has_side_effects=True, vmem_limit_bytes=60 * 2**20),
    )(activations, grads_t)


def solution(mesh):
    return jax.shard_map(
        functools.partial(body, mesh.shape["tok"], mesh.shape["col"]),
        mesh=mesh,
        in_specs=(P(("tok", "col"), "row"), P(None, "col", ("tok", "row"))),
        out_specs=P("tok", "col", "row"),
        check_vma=False,
    )
```

time: 197 us -> 136 us (0.69)
  Pallas kernels: 0 us -> 122 us
  waiting for transfers between devices: 100 us -> 0 us
  blocking collectives: 49.1 us -> 0 us
  matrix products: 22.3 us -> 0 us
  between operations: 13.1 us -> 0.01 us
  local copies, waits for them, and re-layouts: 10.3 us -> 13.8 us
    pallas_call x0 -> x1, Pallas kernels: none -> 122 us  [body(): pl.pallas_call(functools.partial(kernel, n, m), out_shape=jax.ShapeDtypeS...]
    all_gather x3 -> x0, waiting for transfers between devices: 98.9 us -> none  [the longest x1 79.7 us: body(): acts_all = lax.all_gather(acts_all, 'tok', axis=0, tiled=True)]
    all_to_all x1 -> x0, blocking collectives: 49.1 us -> none  [body(): lax.all_to_all(grads_t, 'tok', split_axis=0, concat_axis=0, tiled=True)]
    dot_general x1 -> x0, matrix products: 22.3 us -> none  [body(): tile = jnp.dot(flat, acts_all, preferred_element_type=jnp.float32)]
    unnamed x0 -> x1, local copies, waits for them, and re-layouts: none -> 13.8 us
    all_gather x1 -> x0, local copies, waits for them, and re-layouts: 10.3 us -> none  [body(): mine = lax.all_gather(mine, 'row', axis=1, tiled=False)]
  transfers between devices with their start and end apart: 3 -> 0, of which waited for: 2 -> 0; matrix products, arithmetic and copies ran while one was open for 5% -> 0% of each run, Pallas kernels for 0% -> 0%
where the time goes in v2:
time: 136 us
  Pallas kernels  122 us (90%)
  local copies, waits for them, and re-layouts  13.8 us (10%)
    pallas_call x1, Pallas kernels, body(): pl.pallas_call(functools.partial(kernel, n, m), out_shape=jax.ShapeDtypeS...  122 us
    unnamed x1, local copies, waits for them, and re-layouts  13.8 us

profile of v2, /device:TPU:1, one launch (start us, length us, event | category | flops | bytes accessed | tf_op | source)
XLA Modules:
  0.0 135.6 jit_solution(5140366589509824834)
XLA Ops:
  0.0 121.8 %shard_map.28 = f32[1,1848,2048]{2,1,0:T(8,128)} custom-call(bf16[128,2048]{1,0:T(8,128)(2,1)} %acts.1, bf16[4,1848,256]{2,1,0:T(8,128)(2,1)} %grads.1), custom_call_target="tpu_custom_call" | custom-call | tf_op jit(solution)/shard_map/pallas_call | solution.py:282
  121.8 13.8 %copy.4 = f32[1,1848,2048]{2,1,0:T(8,128)} copy(f32[1,1848,2048]{2,1,0:T(8,128)} %shard_map.28) | data formatting | bytes 30277632

commit v3 on v2

--- a/solution.py
+++ b/solution.py
@@ -16,8 +16,8 @@
     return place + ((place % 4) // 2) * (1 - 2 * (place % 2))
 
 
-def kernel(n, m, acts, grads, out, first, last, held, total,
-           local_sem, zsend, zrecv, rsend, rrecv, gsend, grecv, psend, out_sem):
+def kernel(n, m, acts, grads, every, held, stage, stage_g,
+           local_sem, zsend, zrecv, rsend, rrecv, gsend, grecv, psend):
     k, r, c = lax.axis_index("tok"), lax.axis_index("row"), lax.axis_index("col")
     place = ring_map(k, n)
     rows, wide = acts.shape
@@ -46,16 +46,14 @@
     def span(tok, col):
         return pl.ds(pl.multiple_of((tok * m + col) * rows, rows), rows)
 
-    own = span(k, c)
-    loads = []
-    for q in range(4):
-        dst = (first, last)[q // 2].at[q % 2, own, :]
-        loads.append(pltpu.make_async_copy(acts.at[:, pl.ds(q * quarter, quarter)], dst, local_sem.at[q]))
-    mine = pltpu.make_async_copy(grads.at[k], held.at[k, r], local_sem.at[4])
-    for load in loads[2:] + loads[:2] + [mine]:
-        load.start()
-    for load in loads:
-        load.wait()
+    def at_slot(tok, side):
+        return held.at[:, pl.ds(pl.multiple_of((tok * 2 + side) * chunk, chunk), chunk)]
+
+    own = every.at[span(k, c), :]
+    enter = pltpu.make_async_copy(acts, stage, local_sem.at[0])
+    enter_g = pltpu.make_async_copy(grads.at[k], stage_g, local_sem.at[1])
+    leave = pltpu.make_async_copy(stage, own, local_sem.at[2])
+    leave_g = pltpu.make_async_copy(stage_g, at_slot(k, r), local_sem.at[3])
 
     @pl.when(up & down)
     def _():
@@ -65,21 +63,23 @@
     def _():
         pl.semaphore_wait(barrier, n + 1)
 
-    def z_copy(item, tok, col, way):
-        buf = first if isinstance(item, int) and item == 0 else last
-        where = buf.at[:, span(tok, col), :]
-        return pltpu.make_async_remote_copy(
-            where, where, zsend.at[way, item, col], zrecv.at[item, col],
+    def z_copy(item, tok, col, way, fresh=False):
+        begin = 0 if isinstance(item, int) and item == 0 else 2 * quarter
+        cols = pl.ds(begin, 2 * quarter)
+        where = every.at[span(tok, col), cols]
+        return pltpu.make_async_remote_copy(
+            acts.at[:, cols] if fresh else where, where,
+            zsend.at[way, item, col], zrecv.at[item, col],
             device_id={"col": c + 1 - 2 * way}, device_id_type=MESH)
 
-    def z_start(item, tok):
+    def z_start(item, tok, fresh=False):
         @pl.when(up)
         def _():
-            z_copy(item, tok, c, 0).start()
+            z_copy(item, tok, c, 0, fresh).start()
 
         @pl.when(down)
         def _():
-            z_copy(item, tok, c, 1).start()
+            z_copy(item, tok, c, 1, fresh).start()
 
     def z_round(s, item, tok):
         below, above = c - 1 - s, c + 1 + s
@@ -100,20 +100,22 @@
             def _():
                 z_copy(item, tok, above, 1).start()
 
-    def ring_copy(line, col, offset, half, way):
-        buf = last if isinstance(line, int) and line == m else first
+    def ring_copy(line, col, offset, half, way, fresh=False):
+        begin = 2 * quarter if isinstance(line, int) and line == m else 0
+        cols = pl.ds(begin + half * quarter, quarter)
         tok = member(offset)
-        where = buf.at[half, span(tok, col), :]
-        return pltpu.make_async_remote_copy(
-            where, where, rsend.at[way, line, tok, half], rrecv.at[line, tok, half],
+        where = every.at[span(tok, col), cols]
+        return pltpu.make_async_remote_copy(
+            acts.at[:, cols] if fresh else where, where,
+            rsend.at[way, line, tok, half], rrecv.at[line, tok, half],
             device_id={"tok": member(1 - 2 * way)}, device_id_type=MESH)
 
-    def ring_start(line, col):
+    def ring_start(line, col, fresh=False):
         for half in range(2):
             for way in range(2):
                 which = half if way == 0 else 1 - half
                 if reach[which][way] >= 1:
-                    ring_copy(line, col, 0, which, way).start()
+                    ring_copy(line, col, 0, which, way, fresh).start()
 
     def ring_step(line, col, t):
         for half in range(2):
@@ -143,27 +145,32 @@
     def g_send(j):
         to = (k + j) % n
         return pltpu.make_async_remote_copy(
-            grads.at[to], held.at[k, r], gsend.at[j], grecv.at[k, r],
+            grads.at[to], at_slot(k, r), gsend.at[j], grecv.at[k, r],
             device_id={"tok": to}, device_id_type=MESH)
 
     def g_recv(tok):
-        where = held.at[tok, r]
+        where = at_slot(tok, r)
         return pltpu.make_async_remote_copy(
             where, where, gsend.at[0], grecv.at[tok, r],
             device_id={"row": 1 - r}, device_id_type=MESH)
 
-    def partner(tok, side):
-        where = held.at[tok, side]
-        return pltpu.make_async_remote_copy(
-            where, where, psend.at[tok], grecv.at[tok, side],
+    def partner(tok, side, fresh=False):
+        where = at_slot(tok, side)
+        return pltpu.make_async_remote_copy(
+            grads.at[tok] if fresh else where, where, psend.at[tok], grecv.at[tok, side],
             device_id={"row": 1 - r}, device_id_type=MESH)
 
-    ring_start(m, c)
-    z_start(0, k)
-    z_start(1, k)
-    ring_start(c, c)
-    mine.wait()
-    partner(k, r).start()
+    ring_start(m, c, True)
+    z_start(0, k, True)
+    z_start(1, k, True)
+    ring_start(c, c, True)
+    partner(k, r, True).start()
+    enter.start()
+    enter_g.start()
+    enter.wait()
+    leave.start()
+    enter_g.wait()
+    leave_g.start()
     for t in range(1, hops + 1):
         ring_step(m, c, t)
         if t == 1:
@@ -172,8 +179,6 @@
         z_start(1 + (n - t), member(-t))
         if 2 * t != n:
             z_start(1 + t, member(t))
-        if t == 1:
-            total[...] = jnp.zeros_like(total)
 
     def item_order():
         order = [0]
@@ -189,17 +194,6 @@
         for j in item_order():
             z_round(s, 1 + j, member(j))
 
-    def compute(buf, base, tok, side):
-        at = pl.ds(pl.multiple_of((tok * 2 + side) * chunk, chunk), chunk)
-        step = min(256, quarter)
-        for half in range(2):
-            @pl.loop(0, quarter // step)
-            def _(i):
-                cols = pl.ds(pl.multiple_of(i * step, step), step)
-                outc = pl.ds(pl.multiple_of((base + half) * quarter + i * step, step), step)
-                total[:, outc] += jnp.dot(
-                    held[tok, side], buf[half, at, cols], preferred_element_type=jnp.float32)
-
     @pl.loop(0, m - 2)
     def _(s):
         whole_round(s)
@@ -209,8 +203,6 @@
         g_recv(tok).wait_recv()
         partner(tok, r).start()
 
-    near = (2 * c) // m
-
     @pl.loop(0, m - 1)
     def _(d):
         at_distance(d, functools.partial(ring_step, t=1))
@@ -218,10 +210,6 @@
     @pl.loop(0, n)
     def _(j):
         partner((k + j) % n, 1 - r).wait_recv()
-
-    @pl.loop(0, n)
-    def _(j):
-        compute(last, 2, j, near)
 
     z_round(m - 2, 0, k)
     at_distance(m - 1, ring_start)
@@ -233,17 +221,6 @@
         def _(d):
             at_distance(d, functools.partial(ring_step, t=t))
 
-    @pl.loop(0, n)
-    def _(j):
-        compute(last, 2, j, 1 - near)
-
-    @pl.loop(0, 2 * n)
-    def _(j):
-        compute(first, 0, j // 2, j % 2)
-
-    writes = pltpu.make_async_copy(total, out.at[0], out_sem)
-    writes.start()
-
     for j in range(1, n):
         g_send(j).wait_send()
 
@@ -271,7 +248,8 @@
     z_sent(0, k)
     for j in range(n):
         z_sent(1 + j, member(j))
-    writes.wait()
+    leave.wait()
+    leave_g.wait()
 
 
 def body(n, m, activations, grads_t):
@@ -279,17 +257,18 @@
     rows, wide = activations.shape
     tokens = rows * n * m
     dma = pltpu.SemaphoreType.DMA
-    return pl.pallas_call(
+    every, held = pl.pallas_call(
         functools.partial(kernel, n, m),
-        out_shape=jax.ShapeDtypeStruct((1, units, wide), jnp.float32),
+        out_shape=(
+            jax.ShapeDtypeStruct((tokens, wide), jnp.bfloat16),
+            jax.ShapeDtypeStruct((units, n * 2 * chunk), jnp.bfloat16),
+        ),
         in_specs=[pl.BlockSpec(memory_space=pl.ANY)] * 2,
-        out_specs=pl.BlockSpec(memory_space=pl.ANY),
+        out_specs=[pl.BlockSpec(memory_space=pl.ANY)] * 2,
         scratch_shapes=[
-            pltpu.VMEM((2, tokens, wide // 4), jnp.bfloat16),
-            pltpu.VMEM((2, tokens, wide // 4), jnp.bfloat16),
-            pltpu.VMEM((n, 2, units, chunk), jnp.bfloat16),
-            pltpu.VMEM((units, wide), jnp.float32),
-            dma((5,)),
+            pltpu.VMEM((rows, wide), jnp.bfloat16),
+            pltpu.VMEM((units, chunk), jnp.bfloat16),
+            dma((4,)),
             dma((2, n + 1, m)),
             dma((n + 1, m)),
             dma((2, m + 1, n, 2)),
@@ -297,11 +276,11 @@
             dma((n,)),
             dma((n, 2)),
             dma((n,)),
-            dma,
         ],
         compiler_params=pltpu.CompilerParams(
             collective_id=0, has_side_effects=True, vmem_limit_bytes=60 * 2**20),
     )(activations, grads_t)
+    return jnp.dot(held, every, preferred_element_type=jnp.float32)[None]
 
 
 def solution(mesh):

time: 136 us -> 115 us (0.85)
  Pallas kernels: 122 us -> 93.1 us
  matrix products: 0 us -> 22.2 us
  local copies, waits for them, and re-layouts: 13.8 us -> 0 us
    pallas_call x1, Pallas kernels: 122 us -> 93.1 us  [body(): pl.pallas_call(functools.partial(kernel, n, m), out_shape=(jax.ShapeDtype...]
    dot_general x0 -> x1, matrix products: none -> 22.2 us  [body(): return jnp.dot(held, every, preferred_element_type=jnp.float32)[None]]
    unnamed x1 -> x0, local copies, waits for them, and re-layouts: 13.8 us -> none
where the time goes in v3:
time: 115 us
  Pallas kernels  93.1 us (81%)
  matrix products  22.2 us (19%)
    pallas_call x1, Pallas kernels, body(): pl.pallas_call(functools.partial(kernel, n, m), out_shape=(jax.ShapeDtype...  93.1 us
    dot_general x1, matrix products, body(): return jnp.dot(held, every, preferred_element_type=jnp.float32)[None]  22.2 us

profile of v3, /device:TPU:1, one launch (start us, length us, event | category | flops | bytes accessed | tf_op | source)
XLA Modules:
  0.0 115.3 jit_solution(2143651731753043305)
XLA Ops:
  0.0 93.1 %shard_map.28 = (bf16[2048,2048]{1,0:T(8,128)(2,1)}, bf16[1848,2048]{1,0:T(8,128)(2,1)}) custom-call(bf16[128,2048]{1,0:T(8,128)(2,1)} %acts.1, bf16[4,1848,256]{2,1,0:T(8,128)(2,1)} %grads.1), custom_call_target="tpu_custom_call" | custom-call | tf_op jit(solution)/shard_map/pallas_call | solution.py:260
  93.1 22.2 %convolution_bitcast_fusion = f32[1,1848,2048]{2,1,0:T(8,128)} fusion(bf16[1848,2048]{1,0:T(8,128)(2,1)} %get-tuple-element.7, bf16[2048,2048]{1,0:T(8,128)(2,1)} %get-tuple-element.8), kind=kOutput, calls=%fused_computation | convolution fusion | flops 15502147584 | bytes 31096832 | tf_op jit(solution)/shard_map/dot_general | solution.py:283

commit v4 on v3

--- a/solution.py
+++ b/solution.py
@@ -203,7 +203,7 @@
         g_recv(tok).wait_recv()
         partner(tok, r).start()
 
-    @pl.loop(0, m - 1)
+    @pl.loop(0, m - 2)
     def _(d):
         at_distance(d, functools.partial(ring_step, t=1))
 
@@ -213,6 +213,7 @@
 
     z_round(m - 2, 0, k)
     at_distance(m - 1, ring_start)
+    at_distance(m - 2, functools.partial(ring_step, t=1))
     at_distance(m - 1, functools.partial(ring_step, t=1))
     for j in item_order():
         z_round(m - 2, 1 + j, member(j))

time: 115 us -> 117 us (1.017)
  Pallas kernels: 93.1 us -> 94.5 us
    pallas_call x1, Pallas kernels: 93.1 us -> 94.5 us  [body(): pl.pallas_call(functools.partial(kernel, n, m), out_shape=(jax.ShapeDtype...]
where the time goes in v4:
time: 117 us
  Pallas kernels  94.5 us (81%)
  matrix products  22.2 us (19%)
    pallas_call x1, Pallas kernels, body(): pl.pallas_call(functools.partial(kernel, n, m), out_shape=(jax.ShapeDtype...  94.5 us
    dot_general x1, matrix products, body(): return jnp.dot(held, every, preferred_element_type=jnp.float32)[None]  22.2 us

profile of v4, /device:TPU:1, one launch (start us, length us, event | category | flops | bytes accessed | tf_op | source)
XLA Modules:
  0.0 116.7 jit_solution(12184470711427964302)
XLA Ops:
  0.0 94.5 %shard_map.28 = (bf16[2048,2048]{1,0:T(8,128)(2,1)}, bf16[1848,2048]{1,0:T(8,128)(2,1)}) custom-call(bf16[128,2048]{1,0:T(8,128)(2,1)} %acts.1, bf16[4,1848,256]{2,1,0:T(8,128)(2,1)} %grads.1), custom_call_target="tpu_custom_call" | custom-call | tf_op jit(solution)/shard_map/pallas_call | solution.py:261
  94.5 22.2 %convolution_bitcast_fusion = f32[1,1848,2048]{2,1,0:T(8,128)} fusion(bf16[1848,2048]{1,0:T(8,128)(2,1)} %get-tuple-element.7, bf16[2048,2048]{1,0:T(8,128)(2,1)} %get-tuple-element.8), kind=kOutput, calls=%fused_computation | convolution fusion | flops 15502147584 | bytes 31096832 | tf_op jit(solution)/shard_map/dot_general | solution.py:284
